TPU v7x, 256 devices: a whole 4x4x8 slice. The times are simulated.
256 devices in a mesh: section: 4 (over x), depth: 64 (over z, y, core).
Axes of the slice: x: 4, y: 4, z: 8, core: 2. Of those that a mesh axis runs over, the one named last changes fastest.
Arguments:
- activations: float32 [4, 4, 128, 64, 256], P('section', None, 'depth'), may hold values from -6 to 6
- filters: float32 [4, 27, 64, 64], P('section'), may hold values from -0.15625 to 0.15625
- cotangent: float32 [4, 128, 64, 256], P(None, 'depth'), may hold values from -6 to 6
Outputs:
- input_grads: float32 [4, 4, 128, 64, 256], P('section', None, 'depth')
- filter_grads: float32 [4, 27, 64, 64], P('section')
All inputs are finite; a program needn't handle non-finite values.
Results may differ from a plain program's by a relative error of at most 0.0003.
Values sent between devices are 32-bit elements; how exact they have to be, the bound alone decides.
A program may use at most 128 MiB of HBM per device.

v0:
```python
import math

import jax
import jax.numpy as jnp
from jax import lax
from jax.sharding import Mesh
from jax.sharding import PartitionSpec as P

H = 16
W = 16
DEPTH = ("depth_0", "depth_1", "depth_2")


def padded_2(cells, sides, width):
    for axis, dim in sides:
        count = lax.axis_size(axis)
        ends = count - 1
        head = lax.slice_in_dim(cells, 0, width, axis=dim)
        tail = lax.slice_in_dim(cells, cells.shape[dim] - width, cells.shape[dim], axis=dim)
        cells = jnp.concatenate(
            [
                lax.ppermute(tail, axis, [(i, (i + 1) % count) for i in range(ends)]),
                cells,
                lax.ppermute(head, axis, [((i + 1) % count, i) for i in range(ends)]),
            ],
            axis=dim,
        )
    return cells


def shifted(shard, axis, by):
    size = lax.axis_size(axis)
    pairs = [(i, i + by) for i in range(size) if 0 <= i + by < size]
    return lax.ppermute(shard, axis, pairs)


def filled_up(lines, size):
    spare = -len(lines) % size
    return jnp.pad(lines, [(0, spare)] + [(0, 0)] * (lines.ndim - 1))


def sum_in_order(pieces, axes, sequence):
    dims = [lax.axis_size(a) for a in axes]
    pieces = pieces.reshape(*dims, *pieces.shape[1:])
    pieces = pieces.transpose(*sequence, *range(len(axes), pieces.ndim))
    pieces = pieces.reshape(-1, *pieces.shape[len(axes) :])
    for k in sequence:
        pieces = lax.psum_scatter(pieces, axes[k], scatter_dimension=0, tiled=True)
    return pieces[0]


def all_blocks(shard, axes, sequence):
    pieces = shard[None]
    for k in sequence:
        pieces = lax.all_gather(pieces, axes[k], axis=0, tiled=True)
    carried = [lax.axis_size(axes[k]) for k in reversed(sequence)]
    pieces = pieces.reshape(*carried, *shard.shape)
    turned = sorted(range(len(sequence)), key=lambda place: sequence[len(sequence) - 1 - place])
    return pieces.transpose(*turned, *range(len(sequence), pieces.ndim)).reshape(-1, *shard.shape)


def sum_by_parts(shard, axes, sequence):
    size, lines = (lax.axis_size(axes), shard.reshape(-1, *shard.shape[1:][-1:]))
    pieces = filled_up(lines, size).reshape(size, -1, *lines.shape[1:])
    own = sum_in_order(pieces, axes, sequence)
    whole = all_blocks(own, axes, sequence[::-1]).reshape(-1, *lines.shape[1:])
    return whole[: len(lines)].reshape(shard.shape)


def neighbours(extended, height, breadth):
    planes, channels, columns = extended.shape
    volume_grid = extended.reshape(planes, channels, height, breadth)
    padded = jnp.pad(volume_grid, ((0, 0), (0, 0), (1, 1), (1, 1)))
    pieces = [
        padded[:, :, row_shift : row_shift + height, col_shift : col_shift + breadth]
        for row_shift in range(3)
        for col_shift in range(3)
    ]
    return jnp.stack(pieces, axis=1).reshape(planes, 9, channels, columns)


def apply_taps(patches, kernel_taps, count):
    result = jnp.zeros((count, kernel_taps.shape[2], patches.shape[3]), jnp.float32)
    for plane_shift in range(3):
        result = result + jnp.einsum(
            "koc,dkcp->dop",
            kernel_taps[plane_shift],
            patches[plane_shift : plane_shift + count],
            precision=lax.Precision.HIGHEST,
        )
    return result


def silu_slope(preact):
    sigmoid_value = jax.nn.sigmoid(preact)
    return sigmoid_value * (1.0 + preact * (1.0 - sigmoid_value))


def per_device(activations, filters, cotangent):
    sections = lax.axis_size("section")
    section_index = lax.axis_index("section")
    micro_count = activations.shape[1]
    slab_planes = activations.shape[2]
    channels = activations.shape[3]
    columns = activations.shape[4]
    height = H
    breadth = W
    kernel_taps = filters[0].reshape(3, 9, channels, channels)
    flipped = jnp.flip(filters[0], 0).transpose(0, 2, 1).reshape(3, 9, channels, channels)
    extended_all = padded_2(activations[0], ((DEPTH, 1),), 1)

    def prepare(extended_one):
        patch_one = neighbours(extended_one, height, breadth)
        return (patch_one, silu_slope(apply_taps(patch_one, kernel_taps, slab_planes)))

    patch_store, slope_store = jax.vmap(prepare)(extended_all)

    def advance(tick_count, state_carry):
        incoming, grad_store, filter_sum = state_carry
        micro_index = tick_count - (sections - 1 - section_index)
        active = (micro_index >= 0) & (micro_index < micro_count)
        slot_index = jnp.clip(micro_index, 0, micro_count - 1)
        top_grad = lax.dynamic_index_in_dim(cotangent, slot_index, 0, keepdims=False)
        upstream = jnp.where(section_index == sections - 1, top_grad, incoming)
        patches = lax.dynamic_index_in_dim(patch_store, slot_index, 0, keepdims=False)
        inner_grad = upstream * lax.dynamic_index_in_dim(slope_store, slot_index, 0, keepdims=False)
        slopes = padded_2(inner_grad, ((DEPTH, 0),), 1)
        offset = 0
        backward = apply_taps(neighbours(slopes, height, breadth), flipped, slab_planes)
        own_slopes = slopes[1 : 1 + slab_planes]
        pieces = [
            jnp.einsum(
                "dop,dkcp->koc",
                own_slopes,
                patches[offset + plane_shift : offset + plane_shift + slab_planes],
                precision=lax.Precision.HIGHEST,
            )
            for plane_shift in range(3)
        ]
        filter_term = jnp.where(active, jnp.stack(pieces).reshape(27, channels, channels), 0.0)
        grad_store = jnp.where(
            active, lax.dynamic_update_index_in_dim(grad_store, backward, slot_index, 0), grad_store
        )
        filter_sum = filter_sum + filter_term
        passed = shifted(backward, "section", -1)
        return (passed, grad_store, filter_sum)

    start = (
        jnp.zeros((slab_planes, channels, columns), jnp.float32),
        jnp.zeros((micro_count, slab_planes, channels, columns), jnp.float32),
        jnp.zeros((27, channels, channels), jnp.float32),
    )
    passed, grad_store, filter_sum = lax.fori_loop(0, micro_count + sections - 1, advance, start)
    summed = sum_by_parts(filter_sum, DEPTH, (0, 1, 2))
    scaling = 1.0 / math.sqrt(micro_count * slab_planes * lax.axis_size(DEPTH) * height * breadth)
    return (grad_store[None], (summed * scaling)[None])


def solution(mesh):
    finer = Mesh(
        mesh.devices.reshape(mesh.shape["section"], 8, 4, 2),
        ("section", "depth_0", "depth_1", "depth_2"),
    )
    placed = (
        P("section", None, DEPTH, None, None),
        P("section", None, None, None),
        P(None, DEPTH, None, None),
    )
    return jax.shard_map(
        per_device,
        mesh=finer,
        in_specs=placed,
        out_specs=(P("section", None, DEPTH, None, None), P("section", None, None, None)),
        check_vma=False,
    )
```

profile of v0, /device:TPU:1, one launch (start us, length us, event | category | flops | bytes accessed | tf_op | source)
XLA Modules:
  0.0 456.0 jit_solution(2369570339047331197)
XLA Ops:
  9.1 5.1 %collective-permute-start.4 = (f32[4,1,64,256]{3,2,0,1:T(8,128)S(1)}, f32[4,1,64,256]{3,2,0,1:T(8,128)}, u32[]{:S(2)}, u32[]{:S(2)}) collective-permute-start(f32[4,1,64,256]{3,2,0,1:T(8,128)S(1)} %get-tuple-element.336), channel_id=1, source_target_pairs={{1,0},{2,1},{3,2},{4,3},{5,4},{6,5},{7,6},{8,7},{9,8},{10,9},{11,1... | collective-permute-start | bytes 786440 | tf_op jit(solution)/shard_map/ppermute | solution.py:24
  24.6 5.9 %fusion.48 = (f32[4,4,64,16,16]{2,4,3,1,0:T(8,128)}, f32[4,4,64,16,16]{2,4,3,1,0:T(8,128)}, f32[4,4,64,16,16]{2,4,3,1,0:T(8,128)}, f32[4,4,64,16,16]{2,4,3,1,0:T...) fusion(f32[4,4,64,18,18]{2,4,3,1,0:T(8,128)S(1)} %select_maximu, ...), kind=kLoop, calls=%fused_computation.96 | loop fusion | bytes 16777216 | tf_op jit(solution)/shard_map/vmap()/slice | solution.py:75
  32.8 3.2 copy.74
  35.9 3.2 copy.73
  39.1 3.2 copy.72
  42.3 3.2 copy.71
  45.5 3.2 copy.70
  48.7 3.2 copy.69
  51.9 3.2 copy.68
  61.0 3.4 convolution_bitcast_fusion.3
  64.3 3.4 convolution_bitcast_fusion.4
  67.7 4.4 add_multiply_fusion
  73.7 238.9 %while.20 = (s32[]{:T(128)}, f32[2,64,256]{2,1,0:T(8,128)}, f32[4,2,64,256]{3,2,1,0:T(8,128)}, f32[27,64,64]{1,2,0:T(8,128)S(1)}, pred[]{:T(512)}, /*index=5*/s3...) while((s32[]{:T(128)}, f32[2,64,256]{2,1,0:T(8,128)}, ...), condition=%wide.region_1.2_spmd.clone, body=%wide.region_0.1_spmd.clone.sunk | while | flops 1359802368 | bytes 42467708 | solution.py:153
  76.8 3.1 collective-permute-start
  79.8 2.5 collective-permute-start.1
  82.3 2.2 constant_dynamic-slice_fusion.8
  92.1 2.5 convolution_bitcast_fusion.8
  94.6 2.5 convolution_bitcast_fusion.9
  97.1 4.1 fusion.96
  102.7 4.9 %collective-permute-done.2 = f32[2,64,256]{2,1,0:T(8,128)} collective-permute-done((f32[2,64,256]{2,1,0:T(8,128)S(1)}, f32[2,64,256]{2,1,0:T(8,128)}, u32[]{:S(2)}, u32[]{:S(2)}) %collective-permute-start.2) | collective-permute-done | bytes 131104 | tf_op jit(solution)/shard_map/while/body/eval_jaxpr/ppermute | solution.py:34
  110.7 3.3 collective-permute-start
  114.1 2.2 collective-permute-start.1
  116.3 2.2 constant_dynamic-slice_fusion.8
  126.0 2.5 convolution_bitcast_fusion.8
  128.5 2.5 convolution_bitcast_fusion.9
  131.1 4.1 fusion.96
  136.7 4.7 %collective-permute-done.2 = f32[2,64,256]{2,1,0:T(8,128)} collective-permute-done((f32[2,64,256]{2,1,0:T(8,128)S(1)}, f32[2,64,256]{2,1,0:T(8,128)}, u32[]{:S(2)}, u32[]{:S(2)}) %collective-permute-start.2) | collective-permute-done | bytes 131104 | tf_op jit(solution)/shard_map/while/body/eval_jaxpr/ppermute | solution.py:34
  144.5 3.6 collective-permute-start
  148.1 2.5 collective-permute-start.1
  150.5 2.2 constant_dynamic-slice_fusion.8
  160.2 2.5 convolution_bitcast_fusion.8
  162.8 2.5 convolution_bitcast_fusion.9
  165.3 4.1 fusion.96
  170.9 6.0 %collective-permute-done.2 = f32[2,64,256]{2,1,0:T(8,128)} collective-permute-done((f32[2,64,256]{2,1,0:T(8,128)S(1)}, f32[2,64,256]{2,1,0:T(8,128)}, u32[]{:S(2)}, u32[]{:S(2)}) %collective-permute-start.2) | collective-permute-done | bytes 131104 | tf_op jit(solution)/shard_map/while/body/eval_jaxpr/ppermute | solution.py:34
  180.0 2.8 collective-permute-start
  182.8 2.7 collective-permute-start.1
  185.5 2.2 constant_dynamic-slice_fusion.8
  195.2 2.5 convolution_bitcast_fusion.8
  197.8 2.5 convolution_bitcast_fusion.9
  200.3 4.1 fusion.96
  205.9 5.2 %collective-permute-done.2 = f32[2,64,256]{2,1,0:T(8,128)} collective-permute-done((f32[2,64,256]{2,1,0:T(8,128)S(1)}, f32[2,64,256]{2,1,0:T(8,128)}, u32[]{:S(2)}, u32[]{:S(2)}) %collective-permute-start.2) | collective-permute-done | bytes 131104 | tf_op jit(solution)/shard_map/while/body/eval_jaxpr/ppermute | solution.py:34
  214.1 3.1 collective-permute-start
  217.2 2.5 collective-permute-start.1
  229.4 2.5 convolution_bitcast_fusion.8
  231.9 2.5 convolution_bitcast_fusion.9
  234.5 4.1 fusion.96
  240.1 4.9 %collective-permute-done.2 = f32[2,64,256]{2,1,0:T(8,128)} collective-permute-done((f32[2,64,256]{2,1,0:T(8,128)S(1)}, f32[2,64,256]{2,1,0:T(8,128)}, u32[]{:S(2)}, u32[]{:S(2)}) %collective-permute-start.2) | collective-permute-done | bytes 131104 | tf_op jit(solution)/shard_map/while/body/eval_jaxpr/ppermute | solution.py:34
  248.1 3.4 collective-permute-start
  253.7 2.2 constant_dynamic-slice_fusion.8
  263.4 2.5 convolution_bitcast_fusion.8
  265.9 2.5 convolution_bitcast_fusion.9
  268.4 4.1 fusion.96
  274.0 4.7 %collective-permute-done.2 = f32[2,64,256]{2,1,0:T(8,128)} collective-permute-done((f32[2,64,256]{2,1,0:T(8,128)S(1)}, f32[2,64,256]{2,1,0:T(8,128)}, u32[]{:S(2)}, u32[]{:S(2)}) %collective-permute-start.2) | collective-permute-done | bytes 131104 | tf_op jit(solution)/shard_map/while/body/eval_jaxpr/ppermute | solution.py:34
  281.8 3.6 collective-permute-start
  287.5 2.3 constant_dynamic-slice_fusion.8
  297.3 2.5 convolution_bitcast_fusion.8
  299.8 2.5 convolution_bitcast_fusion.9
  302.3 4.1 fusion.96
  308.0 4.6 %collective-permute-done.2 = f32[2,64,256]{2,1,0:T(8,128)} collective-permute-done((f32[2,64,256]{2,1,0:T(8,128)S(1)}, f32[2,64,256]{2,1,0:T(8,128)}, u32[]{:S(2)}, u32[]{:S(2)}) %collective-permute-start.2) | collective-permute-done | bytes 131104 | tf_op jit(solution)/shard_map/while/body/eval_jaxpr/ppermute | solution.py:34
  314.0 54.1 %reduce-scatter.4.cloned.1.call-done = f32[8,27,64]{2,1,0:T(8,128)} async-done(((f32[64,27,64]{2,1,0:T(8,128)}), f32[8,27,64]{2,1,0:T(8,128)}) %reduce-scatter.4.cloned.1.call-update) | async-done | bytes 55312 | tf_op jit(solution)/shard_map/reduce_scatter | solution.py:48
  368.1 27.0 %reduce-scatter.6.cloned.1.call-done = f32[2,27,64]{2,1,0:T(8,128)} async-done(((f32[8,27,64]{2,1,0:T(8,128)}), f32[2,27,64]{2,1,0:T(8,128)}) %reduce-scatter.6.cloned.1.call-update) | async-done | bytes 13840 | tf_op jit(solution)/shard_map/reduce_scatter | solution.py:48
  395.2 18.0 %reduce-scatter.8.cloned.1.call-done = f32[1,27,64]{2,1,0:T(8,128)} async-done(((f32[2,27,64]{2,1,0:T(8,128)}), f32[1,27,64]{2,1,0:T(8,128)}) %reduce-scatter.8.cloned.1.call-update) | async-done | bytes 6928 | tf_op jit(solution)/shard_map/reduce_scatter | solution.py:48
  415.3 9.5 %all_gather.10 = f32[8,27,64]{2,1,0:T(8,128)S(1)} all-gather(f32[2,27,64]{2,1,0:T(8,128)S(1)} %all_gather.9), channel_id=1, replica_groups=mesh['section'=4,'depth_0'=8,'depth_1'=4,'depth_2'=2] {'depth_1'}, dimensions={0}, use_global_device_ids=true | all-gather | bytes 69120 | tf_op jit(solution)/shard_map/all_gather | solution.py:55
  424.9 23.0 %all_gather.11 = f32[64,27,64]{2,0,1:T(8,128)S(1)} all-gather(f32[8,27,64]{2,0,1:T(8,128)S(1)} %copy.79), channel_id=1, replica_groups=mesh['section'=4,'depth_0'=8,'depth_1'=4,'depth_2'=2] {'depth_0'}, dimensions={0}, use_global_device_ids=true | all-gather | bytes 497664 | tf_op jit(solution)/shard_map/all_gather | solution.py:55
  (233 shorter events, 116.8 us)
Async XLA Ops:
  7.2 10.4 %copy-start.7 = (f32[1,27,64,64]{3,2,1,0:T(8,128)S(1)}, f32[1,27,64,64]{3,2,1,0:T(8,128)}, u32[]{:S(2)}) copy-start(f32[1,27,64,64]{3,2,1,0:T(8,128)} %param.6) | copy-start | bytes 1327108
  7.2 360.9 %reduce-scatter.4.cloned.1.call-start = ((), (), s32[]{:S(2)}) async-start(), calls=%async_computation.3 | async-start | bytes 1179648 | tf_op jit(solution)/shard_map/reduce_scatter | solution.py:48
  9.1 10.9 %collective-permute-start.4 = (f32[4,1,64,256]{3,2,0,1:T(8,128)S(1)}, f32[4,1,64,256]{3,2,0,1:T(8,128)}, u32[]{:S(2)}, u32[]{:S(2)}) collective-permute-start(f32[4,1,64,256]{3,2,0,1:T(8,128)S(1)} %get-tuple-element.336), channel_id=1, source_target_pairs={{1,0},{2,1},{3,2},{4,3},{5,4},{6,5},{7,6},{8,7},{9,8},{10,9},{11,1... | collective-permute-start | bytes 786440 | tf_op jit(solution)/shard_map/ppermute | solution.py:24
  14.2 6.9 %collective-permute-start.3 = (f32[4,1,64,256]{3,2,0,1:T(8,128)}, f32[4,1,64,256]{3,2,0,1:T(8,128)}, u32[]{:S(2)}, u32[]{:S(2)}) collective-permute-start(f32[4,1,64,256]{3,2,0,1:T(8,128)} %get-tuple-element.335), channel_id=1, source_target_pairs={{0,1},{1,2},{2,3},{3,4},{4,5},{5,6},{6,7},{7,8},{8,9},{9,10},{10,1... | collective-permute-start | bytes 786440 | tf_op jit(solution)/shard_map/ppermute | solution.py:22
  55.1 2.9 copy-start.6
  55.1 3.0 copy-start.5
  56.6 1.7 copy-start.1
  58.0 1.6 copy-start.4
  58.1 1.6 copy-start.3
  58.2 1.8 copy-start.2
  59.7 1.2 copy-start.8
  61.0 6.8 %copy-start = (f32[4,4,9,64,256]{4,3,2,1,0:T(8,128)}, f32[4,4,9,64,256]{4,3,2,1,0:T(8,128)S(1)}, u32[]{:S(2)}) copy-start(f32[4,4,9,64,256]{4,3,2,1,0:T(8,128)S(1)} %constant_dynamic-update-slice_fusion.1) | copy-start | bytes 28311556
  76.8 12.9 %collective-permute-start = (f32[1,64,256]{1,2,0:T(8,128)}, f32[1,64,256]{1,2,0:T(8,128)}, u32[]{:S(2)}, u32[]{:S(2)}) collective-permute-start(f32[1,64,256]{1,2,0:T(8,128)} %get-tuple-element.412), channel_id=1, source_target_pairs={{1,0},{2,1},{3,2},{4,3},{5,4},{6,5},{7,6},{8,7},{9,8},{10,9},{11,1... | collective-permute-start | bytes 196616 | tf_op jit(solution)/shard_map/while/body/eval_jaxpr/ppermute | solution.py:24
  79.8 9.8 %collective-permute-start.1 = (f32[1,64,256]{1,2,0:T(8,128)}, f32[1,64,256]{1,2,0:T(8,128)}, u32[]{:S(2)}, u32[]{:S(2)}) collective-permute-start(f32[1,64,256]{1,2,0:T(8,128)} %get-tuple-element.413), channel_id=1, source_target_pairs={{0,1},{1,2},{2,3},{3,4},{4,5},{5,6},{6,7},{7,8},{8,9},{9,10},{10,1... | collective-permute-start | bytes 196616 | tf_op jit(solution)/shard_map/while/body/eval_jaxpr/ppermute | solution.py:22
  101.2 6.5 %collective-permute-start.2 = (f32[2,64,256]{2,1,0:T(8,128)S(1)}, f32[2,64,256]{2,1,0:T(8,128)}, u32[]{:S(2)}, u32[]{:S(2)}) collective-permute-start(f32[2,64,256]{2,1,0:T(8,128)S(1)} %bitcast.305), channel_id=1, source_target_pairs={{64,0},{128,64},{192,128},{65,1},{129,65},{193,129},{66,2},{130,66... | collective-permute-start | bytes 393224 | tf_op jit(solution)/shard_map/while/body/eval_jaxpr/ppermute | solution.py:34
  110.7 12.9 %collective-permute-start = (f32[1,64,256]{1,2,0:T(8,128)}, f32[1,64,256]{1,2,0:T(8,128)}, u32[]{:S(2)}, u32[]{:S(2)}) collective-permute-start(f32[1,64,256]{1,2,0:T(8,128)} %get-tuple-element.412), channel_id=1, source_target_pairs={{1,0},{2,1},{3,2},{4,3},{5,4},{6,5},{7,6},{8,7},{9,8},{10,9},{11,1... | collective-permute-start | bytes 196616 | tf_op jit(solution)/shard_map/while/body/eval_jaxpr/ppermute | solution.py:24
  114.1 9.6 %collective-permute-start.1 = (f32[1,64,256]{1,2,0:T(8,128)}, f32[1,64,256]{1,2,0:T(8,128)}, u32[]{:S(2)}, u32[]{:S(2)}) collective-permute-start(f32[1,64,256]{1,2,0:T(8,128)} %get-tuple-element.413), channel_id=1, source_target_pairs={{0,1},{1,2},{2,3},{3,4},{4,5},{5,6},{6,7},{7,8},{8,9},{9,10},{10,1... | collective-permute-start | bytes 196616 | tf_op jit(solution)/shard_map/while/body/eval_jaxpr/ppermute | solution.py:22
  135.1 6.3 %collective-permute-start.2 = (f32[2,64,256]{2,1,0:T(8,128)S(1)}, f32[2,64,256]{2,1,0:T(8,128)}, u32[]{:S(2)}, u32[]{:S(2)}) collective-permute-start(f32[2,64,256]{2,1,0:T(8,128)S(1)} %bitcast.305), channel_id=1, source_target_pairs={{64,0},{128,64},{192,128},{65,1},{129,65},{193,129},{66,2},{130,66... | collective-permute-start | bytes 393224 | tf_op jit(solution)/shard_map/while/body/eval_jaxpr/ppermute | solution.py:34
  144.5 13.3 %collective-permute-start = (f32[1,64,256]{1,2,0:T(8,128)}, f32[1,64,256]{1,2,0:T(8,128)}, u32[]{:S(2)}, u32[]{:S(2)}) collective-permute-start(f32[1,64,256]{1,2,0:T(8,128)} %get-tuple-element.412), channel_id=1, source_target_pairs={{1,0},{2,1},{3,2},{4,3},{5,4},{6,5},{7,6},{8,7},{9,8},{10,9},{11,1... | collective-permute-start | bytes 196616 | tf_op jit(solution)/shard_map/while/body/eval_jaxpr/ppermute | solution.py:24
  148.1 9.8 %collective-permute-start.1 = (f32[1,64,256]{1,2,0:T(8,128)}, f32[1,64,256]{1,2,0:T(8,128)}, u32[]{:S(2)}, u32[]{:S(2)}) collective-permute-start(f32[1,64,256]{1,2,0:T(8,128)} %get-tuple-element.413), channel_id=1, source_target_pairs={{0,1},{1,2},{2,3},{3,4},{4,5},{5,6},{6,7},{7,8},{8,9},{9,10},{10,1... | collective-permute-start | bytes 196616 | tf_op jit(solution)/shard_map/while/body/eval_jaxpr/ppermute | solution.py:22
  169.4 7.5 %collective-permute-start.2 = (f32[2,64,256]{2,1,0:T(8,128)S(1)}, f32[2,64,256]{2,1,0:T(8,128)}, u32[]{:S(2)}, u32[]{:S(2)}) collective-permute-start(f32[2,64,256]{2,1,0:T(8,128)S(1)} %bitcast.305), channel_id=1, source_target_pairs={{64,0},{128,64},{192,128},{65,1},{129,65},{193,129},{66,2},{130,66... | collective-permute-start | bytes 393224 | tf_op jit(solution)/shard_map/while/body/eval_jaxpr/ppermute | solution.py:34
  180.0 12.9 %collective-permute-start = (f32[1,64,256]{1,2,0:T(8,128)}, f32[1,64,256]{1,2,0:T(8,128)}, u32[]{:S(2)}, u32[]{:S(2)}) collective-permute-start(f32[1,64,256]{1,2,0:T(8,128)} %get-tuple-element.412), channel_id=1, source_target_pairs={{1,0},{2,1},{3,2},{4,3},{5,4},{6,5},{7,6},{8,7},{9,8},{10,9},{11,1... | collective-permute-start | bytes 196616 | tf_op jit(solution)/shard_map/while/body/eval_jaxpr/ppermute | solution.py:24
  182.8 10.1 %collective-permute-start.1 = (f32[1,64,256]{1,2,0:T(8,128)}, f32[1,64,256]{1,2,0:T(8,128)}, u32[]{:S(2)}, u32[]{:S(2)}) collective-permute-start(f32[1,64,256]{1,2,0:T(8,128)} %get-tuple-element.413), channel_id=1, source_target_pairs={{0,1},{1,2},{2,3},{3,4},{4,5},{5,6},{6,7},{7,8},{8,9},{9,10},{10,1... | collective-permute-start | bytes 196616 | tf_op jit(solution)/shard_map/while/body/eval_jaxpr/ppermute | solution.py:22
  204.4 6.7 %collective-permute-start.2 = (f32[2,64,256]{2,1,0:T(8,128)S(1)}, f32[2,64,256]{2,1,0:T(8,128)}, u32[]{:S(2)}, u32[]{:S(2)}) collective-permute-start(f32[2,64,256]{2,1,0:T(8,128)S(1)} %bitcast.305), channel_id=1, source_target_pairs={{64,0},{128,64},{192,128},{65,1},{129,65},{193,129},{66,2},{130,66... | collective-permute-start | bytes 393224 | tf_op jit(solution)/shard_map/while/body/eval_jaxpr/ppermute | solution.py:34
  214.1 12.9 %collective-permute-start = (f32[1,64,256]{1,2,0:T(8,128)}, f32[1,64,256]{1,2,0:T(8,128)}, u32[]{:S(2)}, u32[]{:S(2)}) collective-permute-start(f32[1,64,256]{1,2,0:T(8,128)} %get-tuple-element.412), channel_id=1, source_target_pairs={{1,0},{2,1},{3,2},{4,3},{5,4},{6,5},{7,6},{8,7},{9,8},{10,9},{11,1... | collective-permute-start | bytes 196616 | tf_op jit(solution)/shard_map/while/body/eval_jaxpr/ppermute | solution.py:24
  217.2 9.8 %collective-permute-start.1 = (f32[1,64,256]{1,2,0:T(8,128)}, f32[1,64,256]{1,2,0:T(8,128)}, u32[]{:S(2)}, u32[]{:S(2)}) collective-permute-start(f32[1,64,256]{1,2,0:T(8,128)} %get-tuple-element.413), channel_id=1, source_target_pairs={{0,1},{1,2},{2,3},{3,4},{4,5},{5,6},{6,7},{7,8},{8,9},{9,10},{10,1... | collective-permute-start | bytes 196616 | tf_op jit(solution)/shard_map/while/body/eval_jaxpr/ppermute | solution.py:22
  238.6 6.4 %collective-permute-start.2 = (f32[2,64,256]{2,1,0:T(8,128)S(1)}, f32[2,64,256]{2,1,0:T(8,128)}, u32[]{:S(2)}, u32[]{:S(2)}) collective-permute-start(f32[2,64,256]{2,1,0:T(8,128)S(1)} %bitcast.305), channel_id=1, source_target_pairs={{64,0},{128,64},{192,128},{65,1},{129,65},{193,129},{66,2},{130,66... | collective-permute-start | bytes 393224 | tf_op jit(solution)/shard_map/while/body/eval_jaxpr/ppermute | solution.py:34
  248.1 12.9 %collective-permute-start = (f32[1,64,256]{1,2,0:T(8,128)}, f32[1,64,256]{1,2,0:T(8,128)}, u32[]{:S(2)}, u32[]{:S(2)}) collective-permute-start(f32[1,64,256]{1,2,0:T(8,128)} %get-tuple-element.412), channel_id=1, source_target_pairs={{1,0},{2,1},{3,2},{4,3},{5,4},{6,5},{7,6},{8,7},{9,8},{10,9},{11,1... | collective-permute-start | bytes 196616 | tf_op jit(solution)/shard_map/while/body/eval_jaxpr/ppermute | solution.py:24
  251.4 9.5 %collective-permute-start.1 = (f32[1,64,256]{1,2,0:T(8,128)}, f32[1,64,256]{1,2,0:T(8,128)}, u32[]{:S(2)}, u32[]{:S(2)}) collective-permute-start(f32[1,64,256]{1,2,0:T(8,128)} %get-tuple-element.413), channel_id=1, source_target_pairs={{0,1},{1,2},{2,3},{3,4},{4,5},{5,6},{6,7},{7,8},{8,9},{9,10},{10,1... | collective-permute-start | bytes 196616 | tf_op jit(solution)/shard_map/while/body/eval_jaxpr/ppermute | solution.py:22
  272.5 6.3 %collective-permute-start.2 = (f32[2,64,256]{2,1,0:T(8,128)S(1)}, f32[2,64,256]{2,1,0:T(8,128)}, u32[]{:S(2)}, u32[]{:S(2)}) collective-permute-start(f32[2,64,256]{2,1,0:T(8,128)S(1)} %bitcast.305), channel_id=1, source_target_pairs={{64,0},{128,64},{192,128},{65,1},{129,65},{193,129},{66,2},{130,66... | collective-permute-start | bytes 393224 | tf_op jit(solution)/shard_map/while/body/eval_jaxpr/ppermute | solution.py:34
  281.8 13.1 %collective-permute-start = (f32[1,64,256]{1,2,0:T(8,128)}, f32[1,64,256]{1,2,0:T(8,128)}, u32[]{:S(2)}, u32[]{:S(2)}) collective-permute-start(f32[1,64,256]{1,2,0:T(8,128)} %get-tuple-element.412), channel_id=1, source_target_pairs={{1,0},{2,1},{3,2},{4,3},{5,4},{6,5},{7,6},{8,7},{9,8},{10,9},{11,1... | collective-permute-start | bytes 196616 | tf_op jit(solution)/shard_map/while/body/eval_jaxpr/ppermute | solution.py:24
  285.4 9.5 %collective-permute-start.1 = (f32[1,64,256]{1,2,0:T(8,128)}, f32[1,64,256]{1,2,0:T(8,128)}, u32[]{:S(2)}, u32[]{:S(2)}) collective-permute-start(f32[1,64,256]{1,2,0:T(8,128)} %get-tuple-element.413), channel_id=1, source_target_pairs={{0,1},{1,2},{2,3},{3,4},{4,5},{5,6},{6,7},{7,8},{8,9},{9,10},{10,1... | collective-permute-start | bytes 196616 | tf_op jit(solution)/shard_map/while/body/eval_jaxpr/ppermute | solution.py:22
  306.4 6.1 %collective-permute-start.2 = (f32[2,64,256]{2,1,0:T(8,128)S(1)}, f32[2,64,256]{2,1,0:T(8,128)}, u32[]{:S(2)}, u32[]{:S(2)}) collective-permute-start(f32[2,64,256]{2,1,0:T(8,128)S(1)} %bitcast.305), channel_id=1, source_target_pairs={{64,0},{128,64},{192,128},{65,1},{129,65},{193,129},{66,2},{130,66... | collective-permute-start | bytes 393224 | tf_op jit(solution)/shard_map/while/body/eval_jaxpr/ppermute | solution.py:34
  314.0 81.2 %reduce-scatter.6.cloned.1.call-start = ((), (), s32[]{:S(2)}) async-start(), calls=%async_computation.4 | async-start | bytes 163840 | tf_op jit(solution)/shard_map/reduce_scatter | solution.py:48
  368.1 45.1 %reduce-scatter.8.cloned.1.call-start = ((), (), s32[]{:S(2)}) async-start(), calls=%async_computation.5 | async-start | bytes 49152 | tf_op jit(solution)/shard_map/reduce_scatter | solution.py:48
Sparse Core Ops, SparseCore 0:
  314.1 53.9 reduce-scatter.3
  370.6 24.5 reduce-scatter.5
  397.6 15.5 reduce-scatter.7
where the time goes:
time: 464 us; the launch traced here: 456 us
  waiting for transfers between devices  134 us (29%)
  matrix products  103 us (22%)
  local copies, waits for them, and re-layouts  93.8 us (20%)
  starting transfers between devices  55.5 us (12%)
  blocking collectives  34.6 us (7%)
  other arithmetic  19.5 us (4%)
  between operations  14 us (3%)
    reduce_scatter x3, waiting for transfers between devices, sum_in_order(): pieces = lax.psum_scatter(pieces, axes[k], scatter_dimension=0, tiled=True)  99.1 us
    dot_general x24, matrix products, apply_taps(): jnp.einsum('koc,dkcp->dop', kernel_taps[plane_shift], patches[plane_shift...  75 us
    ppermute x7, waiting for transfers between devices, shifted(): return lax.ppermute(shard, axis, pairs)  35 us
    all_gather x3, blocking collectives, all_blocks(): pieces = lax.all_gather(pieces, axes[k], axis=0, tiled=True)  34.6 us
    ppermute x8, starting transfers between devices, padded_2(): lax.ppermute(head, axis, [((i + 1) % count, i) for i in range(ends)])  27.9 us
    dot_general x21, matrix products, advance(): jnp.einsum('dop,dkcp->koc', own_slopes, patches[offset + plane_shift:offs...  27.8 us
    another operation x16, local copies, waits for them, and re-layouts, neighbours(): return jnp.stack(pieces, axis=1).reshape(planes, 9, channels, columns)  25 us
    ppermute x8, starting transfers between devices, padded_2(): lax.ppermute(tail, axis, [(i, (i + 1) % count) for i in range(ends)])  18.6 us
  transfers between devices with their start and end apart: 26, of which 10 were waited for; matrix products, arithmetic and copies ran while one was open for 13% of the time, Pallas kernels for 0%

commit v1 on v0

v1 whole, which is shorter than its diff:
```python
import functools
import math

import jax
import jax.numpy as jnp
from jax import lax
from jax.experimental import pallas as pl
from jax.experimental.pallas import tpu as pltpu
from jax.sharding import PartitionSpec as P

W = 16
MESH = pl.DeviceIdType.MESH
F32 = jnp.float32
BF16 = jnp.bfloat16


def split(x):
    hi = x.astype(BF16)
    lo = (x - hi.astype(F32)).astype(BF16)
    return hi, lo


def tap_mask(row_step, col_step, cells):
    at = lax.broadcasted_iota(jnp.int32, (1, cells), 1)
    row = at // W + row_step
    col = at % W + col_step
    return (row >= 0) & (row < cells // W) & (col >= 0) & (col < W)


def shifted(x, row_step, col_step):
    if row_step == 0 and col_step == 0:
        return x
    cells = x.shape[-1]
    turned = pltpu.roll(x, (-(row_step * W + col_step)) % cells, 1)
    return jnp.where(tap_mask(row_step, col_step, cells), turned, 0.0)


def kernel(
    grid,
    act, filt, cot, igrad, fgrad,
    wf, wb, halo_a, halo_s, x3, s3, taps, slope, sf, relay, turned, fsum,
    ar, r1, r2, r3, gathered,
    ha_send, ha_recv, hs_send, hs_recv, rel_send, rel_recv,
    c_send, c_recv, y_send, y_recv, z_send, z_recv,
    gz_send, gz_recv, gy_send, gy_recv, gc_send, gc_recv,
):
    nz, ny, nc = grid
    sections = lax.axis_size("section")
    slabs = lax.axis_size("depth")
    s = lax.axis_index("section")
    d = lax.axis_index("depth")
    micro = act.shape[1]
    C = act.shape[3]
    cells = act.shape[4]
    z, y, c = d // (ny * nc), (d // nc) % ny, d % nc
    top = s == sections - 1
    T = 9 * C

    def at_depth(zz, yy, cc):
        return {"depth": (zz * ny + yy) * nc + cc}

    lower, upper = {"depth": d - 1}, {"depth": d + 1}
    y_peers = [at_depth(z, (y + j) % ny, c) for j in range(1, ny)]
    z_peers = [at_depth((z + j) % nz, y, c) for j in range(1, nz)]
    c_peers = [at_depth(z, y, (c + j) % nc) for j in range(1, nc)]

    barrier = pltpu.get_barrier_semaphore()

    def greet(device):
        pl.semaphore_signal(barrier, inc=1, device_id=device, device_id_type=MESH)

    pl.when(d > 0)(lambda: greet(lower))
    pl.when(d < slabs - 1)(lambda: greet(upper))
    pl.when(s > 0)(lambda: greet({"section": s - 1}))
    pl.when(s < sections - 1)(lambda: greet({"section": s + 1}))
    for peer in y_peers + z_peers + c_peers:
        greet(peer)
    expected = (
        (d > 0).astype(jnp.int32)
        + (d < slabs - 1).astype(jnp.int32)
        + (s > 0).astype(jnp.int32)
        + (s < sections - 1).astype(jnp.int32)
        + (nz + ny + nc - 3)
    )
    pl.semaphore_wait(barrier, expected)

    def remote(src, dst, send, recv, device):
        return pltpu.make_async_remote_copy(
            src_ref=src, dst_ref=dst, send_sem=send, recv_sem=recv, device_id=device, device_id_type=MESH
        )

    def face_a(m, side):
        plane, to = (1, upper) if side == 0 else (0, lower)
        return remote(act.at[0, m, plane], halo_a.at[side, m], ha_send.at[side, m], ha_recv.at[side, m], to)

    def face_s(m, side):
        plane, to = (1, upper) if side == 0 else (0, lower)
        return remote(sf.at[m, plane], halo_s.at[side, m], hs_send.at[side, m], hs_recv.at[side, m], to)

    def pass_down(m):
        return remote(igrad.at[0, m], relay.at[m], rel_send.at[m], rel_recv.at[m], {"section": s - 1})

    for m in range(micro):
        pl.when(d > 0)(lambda m=m: face_a(m, 1).start())
        pl.when(d < slabs - 1)(lambda m=m: face_a(m, 0).start())

    none = jnp.zeros((C, C), F32)

    def prepare(t, carry):
        rows0 = pl.ds(pl.multiple_of(t * C, C), C)
        rows1 = pl.ds(pl.multiple_of(T + t * C, C), C)
        f = [filt[0, 9 * a + t] for a in range(3)]
        g = [filt[0, 26 - 9 * a - t].T for a in range(3)]
        for w, b in ((wf, f), (wb, g)):
            for rows, parts in ((rows0, [*b, none]), (rows1, [none, *b])):
                hi, lo = split(jnp.concatenate(parts, axis=1))
                w[rows, : 4 * C] = hi
                w[rows, 4 * C :] = lo
        return carry

    lax.fori_loop(0, 9, prepare, 0)
    fsum[...] = jnp.zeros_like(fsum)
    ar[...] = jnp.zeros_like(ar)

    E = 4 * C

    def put(buf, rows, x):
        hi, lo = split(x)
        lead = rows * C
        return hi, lo, pl.ds(lead, C), pl.ds(E + lead, C)

    def convolve(w, hi, lo, store):
        rhs = jnp.concatenate([hi, hi, lo], axis=0)
        for j in range(2):
            w_hi, w_lo = w[j * T : (j + 1) * T, :E], w[j * T : (j + 1) * T, E:]
            lhs = jnp.concatenate([w_hi, w_lo, w_hi], axis=1)
            taps[j * T : (j + 1) * T, :] = jnp.dot(lhs, rhs, preferred_element_type=F32)
        for j in range(2):
            total = taps[j * T + 4 * C : j * T + 5 * C, :]
            for t in (0, 1, 2, 3, 5, 6, 7, 8):
                total = total + shifted(taps[j * T + t * C : j * T + (t + 1) * C, :], t // 3 - 1, t % 3 - 1)
            store(j, total)

    def preact(m):
        for j in range(2):
            hi, lo = split(act[0, m, j])
            x3[m, (j + 1) * C : (j + 2) * C, :] = hi
            x3[m, E + (j + 1) * C : E + (j + 2) * C, :] = lo
        for side, has in ((0, d > 0), (1, d < slabs - 1)):
            first = 3 * C * side

            @pl.when(has)
            def _():
                face_a(m, side).wait_recv()
                hi, lo = split(halo_a[side, m])
                x3[m, first : first + C, :] = hi
                x3[m, E + first : E + first + C, :] = lo

            @pl.when(jnp.logical_not(has))
            def _():
                x3[m, first : first + C, :] = jnp.zeros((C, cells), BF16)
                x3[m, E + first : E + first + C, :] = jnp.zeros((C, cells), BF16)

        def store(j, total):
            sg = 1.0 / (1.0 + jnp.exp(-total))
            slope[m, j] = sg * (1.0 + total * (1.0 - sg))

        convolve(wf, x3[m, :E, :], x3[m, E:, :], store)

    def first_preacts(m, carry):
        preact(m)
        return carry

    lax.fori_loop(0, jnp.where(top, 1, micro), first_preacts, 0)

    def backward(m, carry):
        @pl.when(top)
        def _():
            sf[m] = cot[m] * slope[m]

        @pl.when(jnp.logical_not(top))
        def _():
            remote(igrad.at[0, m], relay.at[m], rel_send.at[m], rel_recv.at[m], {"section": s}).wait_recv()
            sf[m] = relay[m] * slope[m]

        for j in range(2):
            hi, lo = split(sf[m, j])
            s3[(j + 1) * C : (j + 2) * C, :] = hi
            s3[E + (j + 1) * C : E + (j + 2) * C, :] = lo
        pl.when(d > 0)(lambda: face_s(m, 1).start())
        pl.when(d < slabs - 1)(lambda: face_s(m, 0).start())

        for t in range(9):
            for j in range(2):
                hi, lo = split(shifted(sf[m, j], 1 - t // 3, 1 - t % 3))
                turned[t * C : (t + 1) * C, 2 * j * cells : (2 * j + 1) * cells] = hi
                turned[t * C : (t + 1) * C, (2 * j + 1) * cells : (2 * j + 2) * cells] = lo
        lhs = [turned[:, i * cells : (i + 1) * cells] for i in (0, 1, 0, 2, 3, 2)]
        rhs = [x3[m, first : first + 3 * C, :] for first in (0, 0, E, C, C, E + C)]
        fsum[...] += lax.dot_general(
            jnp.concatenate(lhs, axis=1),
            jnp.concatenate(rhs, axis=1),
            (((1,), (1,)), ((), ())),
            preferred_element_type=F32,
        )

        pl.when(top & (m < micro - 1))(lambda: preact(jnp.minimum(m + 1, micro - 1)))

        for side, has in ((0, d > 0), (1, d < slabs - 1)):
            first = 3 * C * side

            @pl.when(has)
            def _():
                face_s(m, side).wait_recv()
                hi, lo = split(halo_s[side, m])
                s3[first : first + C, :] = hi
                s3[E + first : E + first + C, :] = lo

            @pl.when(jnp.logical_not(has))
            def _():
                s3[first : first + C, :] = jnp.zeros((C, cells), BF16)
                s3[E + first : E + first + C, :] = jnp.zeros((C, cells), BF16)

        def store(j, total):
            igrad[0, m, j] = total

        convolve(wb, s3[:E, :], s3[E:, :], store)
        pl.when(s > 0)(lambda: pass_down(m).start())
        return carry

    lax.fori_loop(0, micro, backward, 0)

    chunks = nz * ny * nc
    rows = ar.shape[1]
    half = T // 2
    ar[: T // rows] = fsum[:, :128].reshape(T // rows, rows, 128)
    ar[T // rows : (T + half) // rows] = jnp.concatenate(
        [fsum[:half, 128:], fsum[half:, 128:]], axis=1
    ).reshape(half // rows, rows, 128)

    per_c, per_y = nz * ny, nz

    def block_c(cc):
        return pl.ds(cc * per_c, per_c)

    def block_y(yy):
        return pl.ds(c * per_c + yy * per_y, per_y)

    mine = c * per_c + y * per_y + z

    to_c = [
        remote(ar.at[block_c((c + j) % nc)], r1.at[j - 1], c_send.at[j - 1], c_recv.at[j - 1], c_peers[j - 1])
        for j in range(1, nc)
    ]
    for copy in to_c:
        copy.start()
    for copy in to_c:
        copy.wait_recv()
    for j in range(nc - 1):
        ar[block_c(c)] += r1[j]

    to_y = [
        remote(ar.at[block_y((y + j) % ny)], r2.at[j - 1], y_send.at[j - 1], y_recv.at[j - 1], y_peers[j - 1])
        for j in range(1, ny)
    ]
    for copy in to_y:
        copy.start()
    for copy in to_y:
        copy.wait_recv()
    total = ar[block_y(y)]
    for j in range(ny - 1):
        total = total + r2[j]
    ar[block_y(y)] = total

    to_z = [
        remote(
            ar.at[c * per_c + y * per_y + (z + j) % nz], r3.at[j - 1], z_send.at[j - 1], z_recv.at[j - 1], z_peers[j - 1]
        )
        for j in range(1, nz)
    ]
    for copy in to_z:
        copy.start()
    for copy in to_z:
        copy.wait_recv()
    total = ar[mine]
    for j in range(nz - 1):
        total = total + r3[j]
    scaling = 1.0 / math.sqrt(micro * 2 * slabs * cells)
    gathered[mine] = total * scaling

    out_z = [
        remote(gathered.at[mine], gathered.at[mine], gz_send.at[j], gz_recv.at[j], z_peers[j]) for j in range(nz - 1)
    ]
    for copy in out_z:
        copy.start()
    for copy in out_z:
        copy.wait_recv()
    out_y = [
        remote(gathered.at[block_y(y)], gathered.at[block_y(y)], gy_send.at[j], gy_recv.at[j], y_peers[j])
        for j in range(ny - 1)
    ]
    for copy in out_y:
        copy.start()
    for copy in out_y:
        copy.wait_recv()
    out_c = [
        remote(gathered.at[block_c(c)], gathered.at[block_c(c)], gc_send.at[j], gc_recv.at[j], c_peers[j])
        for j in range(nc - 1)
    ]
    for copy in out_c:
        copy.start()
    for copy in out_c:
        copy.wait_recv()

    done = gathered[: (T + half) // rows].reshape(T + half, 128)
    last = jnp.concatenate([done[T:, :C], done[T:, C:]], axis=0)
    for t in range(9):
        block = done[t * C : (t + 1) * C, :]
        fgrad[0, t] = block[:, :C]
        fgrad[0, 9 + t] = block[:, C:]
        fgrad[0, 18 + t] = last[t * C : (t + 1) * C, :]

    for copy in to_c + to_y + to_z + out_z + out_y + out_c:
        copy.wait_send()
    for m in range(micro):
        for side, has in ((1, d > 0), (0, d < slabs - 1)):
            pl.when(has)(lambda m=m, side=side: face_a(m, side).wait_send())
            pl.when(has)(lambda m=m, side=side: face_s(m, side).wait_send())
        pl.when(s > 0)(lambda m=m: pass_down(m).wait_send())


def per_device(grid, activations, filters, cotangent):
    micro, planes, C, cells = activations.shape[1:]
    nz, ny, nc = grid
    chunks = nz * ny * nc
    rows = -(-(27 * C * C) // (128 * 8 * chunks)) * 8
    rows = next(r for r in (8, 16, 32, 48, 96, 144, 288) if r >= rows)
    dma = pltpu.SemaphoreType.DMA
    vmem = pl.BlockSpec(memory_space=pltpu.VMEM)
    plane = (C, cells)
    return pl.pallas_call(
        functools.partial(kernel, grid),
        out_shape=(
            jax.ShapeDtypeStruct(activations.shape, F32),
            jax.ShapeDtypeStruct(filters.shape, F32),
        ),
        in_specs=[vmem] * 3,
        out_specs=(vmem, vmem),
        scratch_shapes=[
            pltpu.VMEM((18 * C, 8 * C), BF16),
            pltpu.VMEM((18 * C, 8 * C), BF16),
            pltpu.VMEM((2, micro, *plane), F32),
            pltpu.VMEM((2, micro, *plane), F32),
            pltpu.VMEM((micro, 8 * C, cells), BF16),
            pltpu.VMEM((8 * C, cells), BF16),
            pltpu.VMEM((18 * C, cells), F32),
            pltpu.VMEM((micro, planes, *plane), F32),
            pltpu.VMEM((micro, planes, *plane), F32),
            pltpu.VMEM((micro, planes, *plane), F32),
            pltpu.VMEM((9 * C, 4 * cells), BF16),
            pltpu.VMEM((9 * C, 3 * C), F32),
            pltpu.VMEM((chunks, rows, 128), F32),
            pltpu.VMEM((max(nc - 1, 1), nz * ny, rows, 128), F32),
            pltpu.VMEM((max(ny - 1, 1), nz, rows, 128), F32),
            pltpu.VMEM((max(nz - 1, 1), rows, 128), F32),
            pltpu.VMEM((chunks, rows, 128), F32),
            dma((2, micro)), dma((2, micro)), dma((2, micro)), dma((2, micro)), dma((micro,)), dma((micro,)),
            dma((max(nc - 1, 1),)), dma((max(nc - 1, 1),)), dma((max(ny - 1, 1),)), dma((max(ny - 1, 1),)),
            dma((max(nz - 1, 1),)), dma((max(nz - 1, 1),)), dma((max(nz - 1, 1),)), dma((max(nz - 1, 1),)),
            dma((max(ny - 1, 1),)), dma((max(ny - 1, 1),)), dma((max(nc - 1, 1),)), dma((max(nc - 1, 1),)),
        ],
        compiler_params=pltpu.CompilerParams(
            collective_id=0, has_side_effects=True, vmem_limit_bytes=60 * 1024 * 1024
        ),
    )(activations, filters, cotangent)


def solution(mesh):
    slabs = mesh.shape["depth"]
    grid = (slabs // 8, 4, 2) if slabs >= 32 else (slabs // 4, 2, 2)
    return jax.shard_map(
        functools.partial(per_device, grid),
        mesh=mesh,
        in_specs=(
            P("section", None, "depth", None, None),
            P("section", None, None, None),
            P(None, "depth", None, None),
        ),
        out_specs=(P("section", None, "depth", None, None), P("section", None, None, None)),
        check_vma=False,
    )
```

time: 464 us -> 92.6 us (0.20); the launches traced: 456 us -> 92.5 us
  waiting for transfers between devices: 134 us -> 0 us
  matrix products: 103 us -> 0 us
  local copies, waits for them, and re-layouts: 93.8 us -> 2.86 us
  Pallas kernels: 0 us -> 89 us
  starting transfers between devices: 55.5 us -> 0 us
  blocking collectives: 34.6 us -> 0 us
  other arithmetic: 19.5 us -> 0 us
  between operations: 14 us -> 0.65 us
    dot_general x45 -> x0, matrix products: 103 us -> none  [the longest x24 75 us: apply_taps(): jnp.einsum('koc,dkcp->dop', kernel_taps[plane_shift], patches[plane_shift...]
    reduce_scatter x3 -> x0, waiting for transfers between devices: 99.1 us -> none  [sum_in_order(): pieces = lax.psum_scatter(pieces, axes[k], scatter_dimension=0, tiled=True)]
    pallas_call x0 -> x1, Pallas kernels: none -> 89 us  [per_device(): pl.pallas_call(functools.partial(kernel, grid), out_shape=(jax.ShapeDtype...]
    ppermute x23 -> x0, starting transfers between devices: 55.4 us -> none  [the longest x8 27.9 us: padded_2(): lax.ppermute(head, axis, [((i + 1) % count, i) for i in range(ends)])]
    ppermute x23 -> x0, waiting for transfers between devices: 35 us -> none  [the longest x7 35 us: shifted(): return lax.ppermute(shard, axis, pairs)]
    all_gather x3 -> x0, blocking collectives: 34.6 us -> none  [all_blocks(): pieces = lax.all_gather(pieces, axes[k], axis=0, tiled=True)]
    slice x23 -> x0, local copies, waits for them, and re-layouts: 33.3 us -> none  [the longest x7 15.6 us: advance(): patches[offset + plane_shift:offset + plane_shift + slab_planes]]
    another operation x17 -> x0, local copies, waits for them, and re-layouts: 26.1 us -> none  [the longest x16 25 us: neighbours(): return jnp.stack(pieces, axis=1).reshape(planes, 9, channels, columns)]
  transfers between devices with their start and end apart: 26 -> 0, of which waited for: 10 -> 0; matrix products, arithmetic and copies ran while one was open for 13% -> 0% of each run, Pallas kernels for 0% -> 0%
where the time goes in v1:
time: 92.6 us; the launch traced here: 92.5 us
  Pallas kernels  89 us (96%)
  local copies, waits for them, and re-layouts  2.86 us (3%)
    pallas_call x1, Pallas kernels, per_device(): pl.pallas_call(functools.partial(kernel, grid), out_shape=(jax.ShapeDtype...  89 us
    unnamed x4, local copies, waits for them, and re-layouts  2.86 us

profile of v1, /device:TPU:1, one launch (start us, length us, event | category | flops | bytes accessed | tf_op | source)
XLA Modules:
  0.0 92.5 jit_solution(10741720096778741453)
XLA Ops:
  0.6 89.0 %shard_map.50 = (f32[1,4,2,64,256]{4,3,2,1,0:T(8,128)}, f32[1,27,64,64]{3,2,1,0:T(8,128)}) custom-call(f32[1,4,2,64,256]{4,3,2,1,0:T(8,128)} %act.1, f32[1,27,64,64]{3,2,1,0:T(8,128)} %filt.1, f32[4,2,64,256]{3,2,1,0:T(8,128)} %cot.1), custom_call_target="tpu_custom_call" | custom-call | tf_op jit(solution)/shard_map/pallas_call | solution.py:341
  89.6 0.0 copy-start
  89.7 1.9 %copy.7 = f32[1,4,2,64,256]{4,3,2,1,0:T(8,128)} copy(f32[1,4,2,64,256]{4,3,2,1,0:T(8,128)} %get-tuple-element.4) | data formatting | bytes 1048576
  91.6 0.0 copy-done
  91.6 0.9 copy.8
Async XLA Ops:
  89.6 2.0 %copy-start = (f32[1,27,64,64]{3,2,1,0:T(8,128)S(1)}, f32[1,27,64,64]{3,2,1,0:T(8,128)}, u32[]{:S(2)}) copy-start(f32[1,27,64,64]{3,2,1,0:T(8,128)} %get-tuple-element.5) | copy-start | bytes 1327108

commit v2 on v1

v2 whole, which is shorter than its diff:
```python
import functools
import math

import jax
import jax.numpy as jnp
from jax import lax
from jax.experimental import pallas as pl
from jax.experimental.pallas import tpu as pltpu
from jax.sharding import PartitionSpec as P

W = 16
MESH = pl.DeviceIdType.MESH
F32 = jnp.float32
BF16 = jnp.bfloat16


def split(x):
    hi = x.astype(BF16)
    lo = (x - hi.astype(F32)).astype(BF16)
    return hi, lo


def tap_mask(row_step, col_step, cells):
    at = lax.broadcasted_iota(jnp.int32, (1, cells), 1)
    row = at // W + row_step
    col = at % W + col_step
    return (row >= 0) & (row < cells // W) & (col >= 0) & (col < W)


def shifted(x, row_step, col_step):
    if row_step == 0 and col_step == 0:
        return x
    cells = x.shape[-1]
    turned = pltpu.roll(x, (-(row_step * W + col_step)) % cells, 1)
    return jnp.where(tap_mask(row_step, col_step, cells), turned, 0.0)


def kernel(
    grid,
    act_hbm, filt_hbm, cot_hbm, igrad, fgrad,
    act, filt, cot, wf, wb, halo_a, halo_s, x3, s3, taps, slope, sf, relay, turned, fsum,
    ar, r1, r2, r3, gathered,
    ha_send, ha_recv, hs_send, hs_recv, rel_send, rel_recv,
    c_send, c_recv, y_send, y_recv, z_send, z_recv,
    gz_send, gz_recv, gy_send, gy_recv, gc_send, gc_recv, in_sem, known,
):
    nz, ny, nc = grid
    sections = lax.axis_size("section")
    slabs = lax.axis_size("depth")
    s = lax.axis_index("section")
    d = lax.axis_index("depth")
    micro = act.shape[1]
    C = act.shape[3]
    cells = act.shape[4]
    z, y, c = d // (ny * nc), (d // nc) % ny, d % nc
    top = s == sections - 1
    T = 9 * C
    E = 4 * C
    LO = 5 * C

    def at_depth(zz, yy, cc):
        return {"depth": (zz * ny + yy) * nc + cc}

    outer, inner = c, 1 - c
    across = d - 1 + 2 * c
    has_outer = (across >= 0) & (across < slabs)
    far, near = {"depth": across}, {"depth": d + 1 - 2 * c}
    y_peers = [at_depth(z, (y + j) % ny, c) for j in range(1, ny)]
    z_peers = [at_depth((z + j) % nz, y, c) for j in range(1, nz)]

    loads = [
        pltpu.make_async_copy(src, dst, in_sem.at[k])
        for k, (src, dst) in enumerate(((act_hbm, act), (filt_hbm, filt), (cot_hbm, cot)))
    ]
    for load in loads:
        load.start()

    barrier = pltpu.get_barrier_semaphore()

    def greet(device):
        pl.semaphore_signal(barrier, inc=1, device_id=device, device_id_type=MESH)

    pl.when(has_outer)(lambda: greet(far))
    pl.when(s > 0)(lambda: greet({"section": s - 1}))
    pl.when(s < sections - 1)(lambda: greet({"section": s + 1}))
    y_sides = [at_depth(z, (y + j) % ny, c) for j in (1, ny - 1)]
    z_sides = [at_depth((z + j) % nz, y, c) for j in (1, nz - 1)]
    for peer in [near] + y_sides + z_sides:
        greet(peer)
    expected = (
        has_outer.astype(jnp.int32)
        + (s > 0).astype(jnp.int32)
        + (s < sections - 1).astype(jnp.int32)
        + 5
    )

    def remote(src, dst, send, recv, device):
        return pltpu.make_async_remote_copy(
            src_ref=src, dst_ref=dst, send_sem=send, recv_sem=recv, device_id=device, device_id_type=MESH
        )

    def face_a(m, which):
        plane, to = ((outer, far), (inner, near))[which]
        return remote(act.at[0, m, plane], halo_a.at[which, m], ha_send.at[which], ha_recv.at[which, m], to)

    def face_s(m, which):
        plane, to = ((outer, far), (inner, near))[which]
        return remote(sf.at[m, plane], halo_s.at[which, m], hs_send.at[which], hs_recv.at[which, m], to)

    def pass_down(m, which, to=None):
        plane = (outer, inner)[which]
        return remote(
            igrad.at[0, m, plane], relay.at[m, plane], rel_send.at[which], rel_recv.at[which, m],
            {"section": s - 1 if to is None else to},
        )

    def every(buf, send, recv):
        return remote(buf, buf, send, recv, near)

    def lead(plane):
        return pl.multiple_of(plane * C, C)

    def put(buf, m, plane, x):
        hi, lo = split(x)
        buf[m, pl.ds(lead(plane), C), :] = hi
        buf[m, pl.ds(LO + lead(plane), C), :] = lo

    def tell(r):
        for peer in z_sides + (y_sides if r == 0 else []):
            pl.semaphore_signal(known.at[r], inc=1, device_id=peer, device_id_type=MESH)

    def hear(r):
        pl.semaphore_wait(known.at[r], 4 if r == 0 else 2)

    def send_faces(m):
        pl.when(has_outer)(lambda: face_a(m, 0).start())
        face_a(m, 1).start()

    with jax.named_scope("load_act"):
        loads[0].wait()
    with jax.named_scope("barrier"):
        pl.semaphore_wait(barrier, expected)
    send_faces(0)
    tell(0)

    with jax.named_scope("prepare"):
        edge = jnp.zeros((C, cells), F32)
        for m in range(micro):
            for j in range(2):
                put(x3, m, j + 1, act[0, m, j])
            put(x3, m, 4, edge)
            put(s3, m, 4, edge)
            put(s3, m, 3 * c, edge)
            pl.when(jnp.logical_not(has_outer))(lambda m=m: put(x3, m, 3 * c, edge))
        fsum[...] = jnp.zeros_like(fsum)
        ar[...] = jnp.zeros_like(ar)
        none = jnp.zeros((C, C), F32)
        loads[1].wait()

        def prepare(t, carry):
            rows = pl.ds(pl.multiple_of(t * C, C), C)
            f = [filt[0, 9 * a + t] for a in range(3)]
            g = [filt[0, 26 - 9 * a - t].T for a in range(3)]
            for w, b in ((wf, f), (wb, g)):
                hi, lo = split(jnp.concatenate([*b, none], axis=1))
                w[rows, :E] = hi
                w[rows, E:] = lo
            return carry

        lax.fori_loop(0, 9, prepare, 0)
        loads[2].wait()

    def convolve(w, buf, m, j, slot):
        hi = buf[m, pl.ds(lead(j), E), :]
        lo = buf[m, pl.ds(LO + lead(j), E), :]
        lhs = jnp.concatenate([w[:, :E], w[:, E:], w[:, :E]], axis=1)
        taps[slot] = jnp.dot(lhs, jnp.concatenate([hi, hi, lo], axis=0), preferred_element_type=F32)
        total = taps[slot, 4 * C : 5 * C, :]
        for t in (0, 1, 2, 3, 5, 6, 7, 8):
            total = total + shifted(taps[slot, t * C : (t + 1) * C, :], t // 3 - 1, t % 3 - 1)
        return total

    def preact(m):
        @pl.when(has_outer)
        def _():
            with jax.named_scope("wait_ha"):
                face_a(m, 0).wait_recv()
            put(x3, m, 3 * c, halo_a[0, m])

        face_a(m, 1).wait_recv()
        put(x3, m, 3 * (1 - c), halo_a[1, m])

        @pl.when(m == 0)
        def _():
            for k in range(1, micro):
                send_faces(k)

        with jax.named_scope("pre_conv"):
            for j in range(2):
                total = convolve(wf, x3, m, j, j)
                sg = 1.0 / (1.0 + jnp.exp(-total))
                slope[m, j] = sg * (1.0 + total * (1.0 - sg))

    def first_preacts(m, carry):
        preact(m)
        return carry

    lax.fori_loop(0, jnp.where(top, 1, micro), first_preacts, 0)

    def take(m, which):
        plane = (outer, inner)[which]

        @pl.when(top)
        def _():
            sf[m, plane] = cot[m, plane] * slope[m, plane]

        @pl.when(jnp.logical_not(top))
        def _():
            with jax.named_scope("wait_relay"):
                pass_down(m, which, s).wait_recv()
            sf[m, plane] = relay[m, plane] * slope[m, plane]

        put(s3, m, plane + 1, sf[m, plane])
        if which == 0:
            pl.when(has_outer)(lambda: face_s(m, 0).start())
        else:
            face_s(m, 1).start()

    def filter_terms(m, which):
        plane = (outer, inner)[which]
        with jax.named_scope("fg"):
            for t in range(9):
                hi, lo = split(shifted(sf[m, plane], 1 - t // 3, 1 - t % 3))
                turned[which, t * C : (t + 1) * C, :cells] = hi
                turned[which, t * C : (t + 1) * C, cells:] = lo
            hi, lo = turned[which, :, :cells], turned[which, :, cells:]
            x_hi = x3[m, pl.ds(lead(plane), 3 * C), :]
            x_lo = x3[m, pl.ds(LO + lead(plane), 3 * C), :]
            fsum[...] += lax.dot_general(
                jnp.concatenate([hi, lo, hi], axis=1),
                jnp.concatenate([x_hi, x_hi, x_lo], axis=1),
                (((1,), (1,)), ((), ())),
                preferred_element_type=F32,
            )

    rows = ar.shape[1]
    half = T // 2
    per_c, per_y = nz * ny, nz

    def block_c(cc):
        return pl.ds(cc * per_c, per_c)

    def block_y(yy):
        return pl.ds(c * per_c + yy * per_y, per_y)

    def chunk(yy, j):
        return c * per_c + yy * per_y + (z + j) % nz

    def to_y(i, j):
        return remote(
            ar.at[chunk((y + i) % ny, j)], r2.at[i - 1, j], y_send, y_recv.at[i - 1, j], y_peers[i - 1]
        )

    def to_z(j):
        return remote(ar.at[chunk(y, j)], r3.at[j - 1], z_send, z_recv, z_peers[j - 1])

    by_distance = sorted(range(nz), key=lambda j: min(j, nz - j))
    to_c = remote(ar.at[block_c(1 - c)], r1, c_send, c_recv, near)

    def exchange():
        ar[: T // rows] = fsum[:, :128].reshape(T // rows, rows, 128)
        ar[T // rows : (T + half) // rows] = jnp.concatenate(
            [fsum[:half, 128:], fsum[half:, 128:]], axis=1
        ).reshape(half // rows, rows, 128)
        to_c.start()

    def start_sum():
        with jax.named_scope("to_c"):
            to_c.wait_recv()
        ar[block_c(c)] += r1[...]
        for j in reversed(by_distance):
            for i in range(1, ny):
                to_y(i, j).start()

    def backward(m, carry):
        pl.when(s == 0)(lambda: filter_terms(m, 0))
        take(m, 1)

        @pl.when(s == 0)
        def _():
            filter_terms(m, 1)
            pl.when(m == micro - 1)(exchange)

        with jax.named_scope("wait_hs1"):
            face_s(m, 1).wait_recv()
        put(s3, m, 3 * (1 - c), halo_s[1, m])
        with jax.named_scope("conv1"):
            igrad[0, m, inner] = convolve(wb, s3, m, inner, 1)
        pl.when((m == micro - 1) & (s == 0))(start_sum)

        @pl.when(m < micro - 1)
        def _():
            pl.when(top)(lambda: preact(m + 1))
            take(m + 1, 0)

        @pl.when(has_outer)
        def _():
            with jax.named_scope("wait_hs0"):
                face_s(m, 0).wait_recv()
            put(s3, m, 3 * c, halo_s[0, m])

        with jax.named_scope("conv0"):
            igrad[0, m, outer] = convolve(wb, s3, m, outer, 0)

        @pl.when(s > 0)
        def _():
            pass_down(m, 0).start()
            pass_down(m, 1).start()

        for r in range(3):

            @pl.when(m == r)
            def _():
                hear(r)
                if r < 2:
                    tell(r + 1)

        return carry

    take(0, 0)
    lax.fori_loop(0, micro, backward, 0)

    @pl.when(s > 0)
    def _():
        def terms(m, carry):
            filter_terms(m, 0)
            filter_terms(m, 1)
            return carry

        lax.fori_loop(0, micro, terms, 0)
        exchange()
        start_sum()

    for j in reversed(by_distance):
        with jax.named_scope("to_y"):
            for i in range(1, ny):
                to_y(i, j).wait_recv()
        total = ar[chunk(y, j)]
        for i in range(1, ny):
            total = total + r2[i - 1, j]
        if j > 0:
            ar[chunk(y, j)] = total
            to_z(j).start()
    with jax.named_scope("to_z"):
        every(r3, z_send, z_recv).wait_recv()
    for j in range(1, nz):
        total = total + r3[j - 1]
    scaling = 1.0 / math.sqrt(micro * 2 * slabs * cells)
    mine = chunk(y, 0)
    gathered[mine] = total * scaling

    def out_z(j):
        return remote(gathered.at[mine], gathered.at[mine], gz_send, gz_recv.at[j - 1], z_peers[j - 1])

    def out_y(i, j):
        at = chunk(y, nz - j)
        return remote(gathered.at[at], gathered.at[at], gy_send, gy_recv.at[i - 1], y_peers[i - 1])

    def out_c(i):
        at = block_y((y + i) % ny)
        return remote(gathered.at[at], gathered.at[at], gc_send, gc_recv, near)

    for j in reversed(by_distance):
        if j > 0:
            out_z(j).start()
    with jax.named_scope("out_z"):
        for j in by_distance:
            if j > 0:
                out_z(j).wait_recv()
            for i in range(1, ny):
                out_y(i, j).start()
    out_c(0).start()
    with jax.named_scope("out_y"):
        for i in range(1, ny):
            every(gathered.at[block_y((y + ny - i) % ny)], gy_send, gy_recv.at[i - 1]).wait_recv()
            out_c(ny - i).start()
    with jax.named_scope("out_c"):
        every(r1, gc_send, gc_recv).wait_recv()

    with jax.named_scope("unpack"):
        done = gathered[: (T + half) // rows].reshape(T + half, 128)
        last = jnp.concatenate([done[T:, :C], done[T:, C:]], axis=0)
        for t in range(9):
            block = done[t * C : (t + 1) * C, :]
            fgrad[0, t] = block[:, :C]
            fgrad[0, 9 + t] = block[:, C:]
            fgrad[0, 18 + t] = last[t * C : (t + 1) * C, :]

    to_c.wait_send()
    every(r2, y_send, c_recv).wait_send()
    every(r3, z_send, c_recv).wait_send()
    every(r3, gz_send, c_recv).wait_send()
    every(r2, gy_send, c_recv).wait_send()
    every(r1, gc_send, c_recv).wait_send()
    for which in range(2):

        def sent(which=which):
            every(halo_a.at[which], ha_send.at[which], c_recv).wait_send()
            every(halo_s.at[which], hs_send.at[which], c_recv).wait_send()

        pl.when(has_outer)(sent) if which == 0 else sent()
        pl.when(s > 0)(lambda which=which: every(halo_s.at[which], rel_send.at[which], c_recv).wait_send())


def per_device(grid, activations, filters, cotangent):
    micro, planes, C, cells = activations.shape[1:]
    nz, ny, nc = grid
    chunks = nz * ny * nc
    rows = -(-(27 * C * C) // (128 * 8 * chunks)) * 8
    rows = next(r for r in (8, 16, 32, 48, 96, 144, 288) if r >= rows)
    dma = pltpu.SemaphoreType.DMA
    vmem = pl.BlockSpec(memory_space=pltpu.VMEM)
    plane = (C, cells)
    return pl.pallas_call(
        functools.partial(kernel, grid),
        out_shape=(
            jax.ShapeDtypeStruct(activations.shape, F32),
            jax.ShapeDtypeStruct(filters.shape, F32),
        ),
        in_specs=[pl.BlockSpec(memory_space=pltpu.HBM)] * 3,
        out_specs=(vmem, vmem),
        scratch_shapes=[
            pltpu.VMEM(activations.shape, F32),
            pltpu.VMEM(filters.shape, F32),
            pltpu.VMEM(cotangent.shape, F32),
            pltpu.VMEM((9 * C, 8 * C), BF16),
            pltpu.VMEM((9 * C, 8 * C), BF16),
            pltpu.VMEM((2, micro, *plane), F32),
            pltpu.VMEM((2, micro, *plane), F32),
            pltpu.VMEM((micro, 10 * C, cells), BF16),
            pltpu.VMEM((micro, 10 * C, cells), BF16),
            pltpu.VMEM((2, 9 * C, cells), F32),
            pltpu.VMEM((micro, planes, *plane), F32),
            pltpu.VMEM((micro, planes, *plane), F32),
            pltpu.VMEM((micro, planes, *plane), F32),
            pltpu.VMEM((2, 9 * C, 2 * cells), BF16),
            pltpu.VMEM((9 * C, 3 * C), F32),
            pltpu.VMEM((chunks, rows, 128), F32),
            pltpu.VMEM((nz * ny, rows, 128), F32),
            pltpu.VMEM((max(ny - 1, 1), nz, rows, 128), F32),
            pltpu.VMEM((max(nz - 1, 1), rows, 128), F32),
            pltpu.VMEM((chunks, rows, 128), F32),
            dma((2,)), dma((2, micro)), dma((2,)), dma((2, micro)), dma((2,)), dma((2, micro)),
            dma, dma, dma, dma((ny - 1, nz)), dma, dma, dma, dma((nz - 1,)), dma, dma((ny - 1,)), dma, dma, dma((3,)),
            pltpu.SemaphoreType.REGULAR((3,)),
        ],
        compiler_params=pltpu.CompilerParams(
            collective_id=0, has_side_effects=True, vmem_limit_bytes=32 * 1024 * 1024
        ),
    )(*(pltpu.with_memory_space_constraint(x, pltpu.HBM) for x in (activations, filters, cotangent)))


def solution(mesh):
    slabs = mesh.shape["depth"]
    grid = (slabs // 8, 4, 2) if slabs >= 32 else (slabs // 4, 2, 2)
    return jax.shard_map(
        functools.partial(per_device, grid),
        mesh=mesh,
        in_specs=(
            P("section", None, "depth", None, None),
            P("section", None, None, None),
            P(None, "depth", None, None),
        ),
        out_specs=(P("section", None, "depth", None, None), P("section", None, None, None)),
        check_vma=False,
    )
```

time: 92.6 us -> 75.6 us (0.82)
  Pallas kernels: 89 us -> 73.2 us
  local copies, waits for them, and re-layouts: 2.86 us -> 1.71 us
    pallas_call x1, Pallas kernels: 89 us -> 73.2 us  [per_device(): pl.pallas_call(functools.partial(kernel, grid), out_shape=(jax.ShapeDtype...]
    unnamed x4 -> x2, local copies, waits for them, and re-layouts: 2.86 us -> 1.71 us
where the time goes in v2:
time: 75.6 us; the launch traced here: 75.5 us
  Pallas kernels  73.2 us (97%)
  local copies, waits for them, and re-layouts  1.71 us (2%)
    pallas_call x1, Pallas kernels, per_device(): pl.pallas_call(functools.partial(kernel, grid), out_shape=(jax.ShapeDtype...  73.2 us
    unnamed x2, local copies, waits for them, and re-layouts  1.71 us

profile of v2, /device:TPU:1, one launch (start us, length us, event | category | flops | bytes accessed | tf_op | source)
XLA Modules:
  0.0 75.5 jit_solution(15447771951654152762)
XLA Ops:
  0.6 73.2 %shard_map.50 = (f32[1,4,2,64,256]{4,3,2,1,0:T(8,128)S(1)}, f32[1,27,64,64]{3,2,1,0:T(8,128)S(1)}) custom-call(f32[1,4,2,64,256]{4,3,2,1,0:T(8,128)} %act_hbm.1, f32[1,27,64,64]{3,2,1,0:T(8,128)} %filt_hbm.1, f32[4,2,64,256]{3,2,1,0:T(8,128)} %cot_hbm.1), custom_call_target="tpu_custom_call" | custom-call | tf_op jit(solution)/shard_map/pallas_call | solution.py:424
  73.8 0.8 %copy.7 = f32[1,4,2,64,256]{4,3,2,1,0:T(8,128)} copy(f32[1,4,2,64,256]{4,3,2,1,0:T(8,128)S(1)} %get-tuple-element.4) | data formatting | bytes 1048576
  74.6 0.9 %copy.8 = f32[1,27,64,64]{3,2,1,0:T(8,128)} copy(f32[1,27,64,64]{3,2,1,0:T(8,128)S(1)} %get-tuple-element.5) | data formatting | bytes 884736
